TPU v7x, 256 devices: a whole 4x4x8 slice. The times are simulated.
256 devices in a mesh: row: 32 (over y, z_hi, core), col: 8 (over z_lo, x).
Axes of the slice: x: 4, y: 4, z: 8 (z_hi: 4, z_lo: 2; z = z_hi * 2 + z_lo), core: 2. Of those that a mesh axis runs over, the one named last changes fastest.
Arguments:
- alignment: bfloat16 [64, 1024, 64], P(None, ('col', 'row')), may hold values from -6 to 6
- pair_rep: bfloat16 [1024, 1024, 128], P('row', 'col'), may hold values from -128 to 128
- outer_left: bfloat16 [64, 32], replicated, may hold values from -0.75 to 0.75
- outer_right: bfloat16 [64, 32], replicated, may hold values from -0.75 to 0.75
- outer_proj: bfloat16 [1024, 128], replicated, may hold values from -1.5 to 1.5
- outer_bias: float32 [128], replicated, may hold values from -3 to 3
- average_value: bfloat16 [64, 256], replicated, may hold values from -0.75 to 0.75
- average_gate: bfloat16 [64, 256], replicated, may hold values from -0.75 to 0.75
- average_logit: bfloat16 [128, 8], replicated, may hold values from -28 to 28
- average_out: bfloat16 [256, 64], replicated, may hold values from -1 to 1
- triangle_proj: bfloat16 [128, 512], replicated, may hold values from -0.5 to 0.5
- triangle_bias: bfloat16 [128, 4], replicated, may hold values from -0.5 to 0.5
Outputs:
- pair_new: bfloat16 [1024, 1024, 128], P('row', 'col')
- alignment_update: bfloat16 [64, 1024, 64], P(None, ('row', 'col'))
- triangle_inputs: bfloat16 [1024, 1024, 512], P(('col', 'row'))
- edge_bias: bfloat16 [4, 1024, 1024], P(None, ('col', 'row'))
All inputs are finite; a program needn't handle non-finite values.
Results may differ from a plain program's by a relative error of at most 0.02.
The roundings to bfloat16 on the way count: a program that leaves them out, or rounds other values in their place, can miss the bound.
Values may be sent and summed in bfloat16 or wider, within the bound.
No kernel may reach another device: no remote copies, remote signals or barrier semaphores. Data moves between devices by JAX's collectives and lax.ppermute only.
A program may use at most 64 MiB of HBM per device.

v0:
```python
import jax
import jax.numpy as jnp
from jax import lax
from jax.sharding import PartitionSpec as P


def broadcast(shard, axis, root):
    mine = lax.axis_index(axis) == root
    return lax.psum(jnp.where(mine, shard, jnp.zeros_like(shard)), axis)


def standardize(values):
    widened = values.astype(jnp.float32)
    centered = widened - jnp.mean(widened, axis=-1, keepdims=True)
    spread = jnp.mean(centered * centered, axis=-1, keepdims=True)
    return centered * lax.rsqrt(spread + 1e-05)


def per_device(
    alignment,
    pair_rep,
    outer_left,
    outer_right,
    outer_proj,
    outer_bias,
    average_value,
    average_gate,
    average_logit,
    average_out,
    triangle_proj,
    triangle_bias,
):
    row_devices = lax.axis_size("row")
    col_devices = lax.axis_size("col")
    local_row_index = lax.axis_index("row")
    col_index = lax.axis_index("col")
    sequence_count, slab_length, alignment_channel_width = alignment.shape
    row_window, cols_tile, pair_width = pair_rep.shape
    factor_width = outer_left.shape[1]
    head_count = average_logit.shape[1]
    value_width = average_value.shape[1]
    head_width = value_width // head_count
    alignment_layer_norm = standardize(alignment).astype(jnp.bfloat16)
    normalized_flat_rows = alignment_layer_norm.reshape(
        sequence_count, slab_length * alignment_channel_width
    )
    right_own = jnp.dot(
        alignment_layer_norm, outer_right, preferred_element_type=jnp.float32
    ).astype(jnp.bfloat16)
    value_own = jnp.dot(
        alignment_layer_norm, average_value, preferred_element_type=jnp.float32
    ).astype(jnp.bfloat16)
    normalized_columns, right_cols, value_cols = (
        lax.all_gather(normalized_flat_rows, "row", axis=1, tiled=True),
        lax.all_gather(
            right_own.reshape(sequence_count, slab_length * factor_width), "row", axis=1, tiled=True
        ),
        lax.all_gather(
            value_own.reshape(sequence_count, slab_length * value_width), "row", axis=1, tiled=True
        ),
    )
    right_cols = right_cols.reshape(sequence_count, cols_tile, factor_width)
    value_cols = value_cols.reshape(sequence_count, cols_tile, value_width)
    group_member_count = row_devices // col_devices
    start_position = local_row_index % group_member_count * (row_window * alignment_channel_width)
    local_rows = lax.dynamic_slice_in_dim(
        normalized_columns, start_position, row_window * alignment_channel_width, 1
    )
    norm_rows = broadcast(local_rows, "col", local_row_index // group_member_count).reshape(
        sequence_count, row_window, alignment_channel_width
    )
    left_rows = jnp.dot(norm_rows, outer_left, preferred_element_type=jnp.float32).astype(
        jnp.bfloat16
    )
    row_block = 8
    block_count = row_window // row_block
    left_blocks = jnp.transpose(
        left_rows.reshape(sequence_count, block_count, row_block * factor_width), (1, 0, 2)
    )
    right_flat = right_cols.reshape(sequence_count, cols_tile * factor_width)

    def pair_block(block_items):
        left_flat, pair_rows = block_items
        outer_sum = lax.dot_general(
            left_flat, right_flat, (((0,), (0,)), ((), ())), preferred_element_type=jnp.float32
        )
        outer_sum = jnp.transpose(
            outer_sum.reshape(row_block, factor_width, cols_tile, factor_width), (0, 2, 1, 3)
        )
        outer_mean = (
            outer_sum.reshape(row_block, cols_tile, factor_width * factor_width) / sequence_count
        ).astype(jnp.bfloat16)
        update = jnp.dot(outer_mean, outer_proj, preferred_element_type=jnp.float32)
        return (pair_rows.astype(jnp.float32) + update + outer_bias).astype(jnp.bfloat16)

    pair_new = lax.map(
        pair_block, (left_blocks, pair_rep.reshape(block_count, row_block, cols_tile, pair_width))
    )
    pair_new = pair_new.reshape(row_window, cols_tile, pair_width)
    pair_norm = standardize(pair_new).astype(jnp.bfloat16)
    logits = jnp.einsum("ijc,ch->hij", pair_norm, average_logit, preferred_element_type=jnp.float32)
    peak_values = lax.pmax(jnp.max(logits, axis=2), "col")
    weights = jnp.exp(logits - peak_values[:, :, None]).astype(jnp.bfloat16)
    denom_part = jnp.sum(weights.astype(jnp.float32), axis=2)
    value_heads = value_cols.reshape(sequence_count, cols_tile, head_count, head_width)
    numer_part = jnp.einsum(
        "hij,sjhc->ishc", weights, value_heads, preferred_element_type=jnp.float32
    )
    numer_part = numer_part.reshape(row_window, sequence_count, value_width)
    out_wide = average_out.astype(jnp.float32)
    numer_sub, denom_sub = (
        lax.psum_scatter(
            numer_part.astype(jnp.bfloat16), "col", scatter_dimension=0, tiled=True
        ).astype(jnp.float32),
        lax.psum_scatter(
            denom_part.astype(jnp.bfloat16), "col", scatter_dimension=1, tiled=True
        ).astype(jnp.float32),
    )
    sub_len = numer_sub.shape[0]
    norm_sub = lax.dynamic_slice_in_dim(norm_rows, col_index * sub_len, sub_len, 1)
    gate_vals = jax.nn.sigmoid(jnp.dot(norm_sub, average_gate, preferred_element_type=jnp.float32))
    gate_vals = gate_vals.reshape(sequence_count, sub_len, head_count, head_width)
    numer_moved = jnp.transpose(
        numer_sub.reshape(sub_len, sequence_count, head_count, head_width), (1, 0, 2, 3)
    )
    gated_vals = (gate_vals * numer_moved / jnp.transpose(denom_sub)[None, :, :, None]).reshape(
        sequence_count, sub_len, value_width
    )
    alignment_update = jnp.dot(gated_vals, out_wide, precision=lax.Precision.HIGHEST).astype(
        jnp.bfloat16
    )
    piece_len = cols_tile // row_devices
    shaped = pair_norm.reshape(row_window, row_devices, piece_len, pair_width)
    split_at = 3 * (triangle_proj.shape[1] // 4)
    turned = lax.all_to_all(shaped, "row", split_axis=1, concat_axis=0, tiled=True)[:, 0]
    projected = jnp.einsum("jic,cd->ijd", turned, triangle_proj, preferred_element_type=jnp.float32)
    inputs = jnp.concatenate(
        [projected[..., :split_at], jax.nn.sigmoid(projected[..., split_at:])], axis=-1
    ).astype(jnp.bfloat16)
    bias_rows = jnp.einsum(
        "jic,ch->ihj", turned, triangle_bias, preferred_element_type=jnp.float32
    ).astype(jnp.bfloat16)
    triangle_inputs, bias_rows = (inputs, bias_rows)
    edge_bias = jnp.transpose(bias_rows, (1, 0, 2))
    return (pair_new, alignment_update, triangle_inputs, edge_bias)


def solution(mesh):
    placed = (
        P(None, ("col", "row"), None),
        P("row", "col", None),
        P(),
        P(),
        P(),
        P(),
        P(),
        P(),
        P(),
        P(),
        P(),
        P(),
    )
    return jax.shard_map(
        per_device,
        mesh=mesh,
        in_specs=placed,
        out_specs=(
            P("row", "col", None),
            P(None, ("row", "col"), None),
            P(("col", "row"), None, None),
            P(None, ("col", "row"), None),
        ),
        check_vma=False,
    )
```

profile of v0, /device:TPU:16, one launch (start us, length us, event | category | flops | bytes accessed | tf_op | source)
XLA Modules:
  0.0 337.7 jit_solution(5402792686740338694)
XLA Ops:
  8.2 1.1 fusion.22
  11.2 53.5 %all-gather.3.cloned.1.call-done = bf16[64,8192]{1,0:T(8,128)(2,1)} async-done(((bf16[64,256]{1,0:T(8,128)(2,1)}), bf16[64,8192]{1,0:T(8,128)(2,1)}) %all-gather.3.cloned.1.call-update) | async-done | bytes 1048592 | tf_op jit(solution)/shard_map/all_gather | solution.py:54
  68.4 41.0 %all_gather.10 = bf16[64,4096]{0,1:T(8,128)(2,1)S(1)} all-gather(bf16[64,128]{0,1:T(8,128)(2,1)S(1)} %bitcast.144), channel_id=1, replica_groups=mesh['row'=32,'col'=8] {'row'}, dimensions={1}, use_global_device_ids=true | all-gather | bytes 540672 | tf_op jit(solution)/shard_map/all_gather | solution.py:55
  109.4 37.8 %all-reduce.3.cloned.1.call-done = bf16[64,32,64]{2,0,1:T(8,128)(2,1)} async-done(((bf16[64,32,64]{2,0,1:T(8,128)(2,1)}), bf16[64,32,64]{2,0,1:T(8,128)(2,1)}) %all-reduce.3.cloned.1.call-update) | async-done | bytes 262160 | tf_op jit(solution)/shard_map/psum | solution.py:9
  147.1 1.6 convolution_convert_fusion
  148.8 17.9 %while.10 = (s32[]{:T(128)}, bf16[4,8,128,128]{3,2,1,0:T(8,128)(2,1)S(1)}, bf16[4,8,128,128]{3,2,1,0:T(8,128)(2,1)}, bf16[4,64,256]{1,2,0:T(8,128)(2,1)S(1)}, bf...) while((s32[]{:T(128)}, ...), condition=%wide.region_4.5_spmd, body=%wide.region_3.4_spmd.sunk | while | flops 405274624 | bytes 10846821 | solution.py:96
  148.8 1.1 copy.111
  151.4 1.8 fusion.60
  153.3 1.1 copy.111
  155.9 1.8 fusion.60
  157.8 1.1 copy.111
  160.4 1.8 fusion.60
  162.2 1.1 copy.111
  164.9 1.8 fusion.60
  166.7 1.9 copy.86
  169.2 1.3 multiply_reduce_fusion
  171.0 3.3 multiply_convert_fusion.1
  174.3 9.3 %all-to-all-start = ((bf16[32,32,4,128]{3,0,2,1:T(8,128)(2,1)}), bf16[32,32,4,128]{3,0,2,1:T(8,128)(2,1)S(1)}, u32[]{:S(2)}, u32[]{:S(2)}) async-start(bf16[32,32,4,128]{3,0,2,1:T(8,128)(2,1)} %multiply_convert_fusion.1), calls=%async_computation.1 | async-start | bytes 2097152 | tf_op jit(solution)/shard_map/all_to_all | solution.py:135
  183.6 2.1 fusion.41
  185.7 55.5 %pmax.7 = f32[8,32]{0,1:T(8,128)S(1)} all-reduce(f32[8,32]{0,1:T(8,128)S(1)} %get-tuple-element.76), channel_id=1, replica_groups=mesh['row'=32,'col'=8] {'col'}, use_global_device_ids=true, to_apply=%region_8.9 | all-reduce | flops 256 | bytes 2048 | tf_op jit(solution)/shard_map/pmax | solution.py:102
  241.4 8.4 %copy.81 = bf16[64,32768]{0,1:T(8,128)(2,1)} copy(bf16[64,32768]{1,0:T(8,128)(2,1)} %all-gather.5.cloned.1.call-done) | data formatting | bytes 8388608 | tf_op jit(solution)/shard_map/all_gather | solution.py:58
  249.8 14.8 %copy.82 = bf16[64,128,8,32]{1,3,0,2:T(8,128)(2,1)} copy(bf16[64,128,8,32]{0,3,2,1:T(8,128)(2,1)} %bitcast.130) | data formatting | bytes 8388608 | tf_op jit(solution)/shard_map/reshape;reshape | solution.py:105
  264.6 5.4 %convert_bitcast_fusion = bf16[32,64,8,32]{0,3,1,2:T(8,128)(2,1)} fusion(bf16[64,128,8,32]{1,3,0,2:T(8,128)(2,1)} %copy.82, bf16[8,32,128,1]{2,0,1,3:T(8,128)(2,1)S(1)} %fusion.33), kind=kOutput, calls=%fused_computation.12 | convolution fusion | flops 134742016 | bytes 5308416 | tf_op jit(solution)/shard_map/hij,sjhc->ishc/dot_general | solution.py:106
  269.9 8.1 %copy.84 = bf16[32,64,8,32]{1,3,2,0:T(8,128)(2,1)} copy(bf16[32,64,8,32]{0,3,1,2:T(8,128)(2,1)} %convert_bitcast_fusion) | data formatting | bytes 2097152 | tf_op jit(solution)/shard_map/convert_element_type | solution.py:113
  280.0 1.0 fusion.13
  281.4 18.6 %all-reduce = bf16[8,32]{0,1:T(8,128)(2,1)S(1)} all-reduce(bf16[8,32]{0,1:T(8,128)(2,1)S(1)} %fusion.32), channel_id=3, replica_groups=mesh['row'=32,'col'=8] {'col'}, use_global_device_ids=true, to_apply=%region_11.12.clone | all-reduce | flops 256 | bytes 1024
  301.1 1.3 copy.89
  302.4 1.3 convolution_bitcast_fusion
  304.8 2.4 pad_maximum_fusion
  307.1 6.2 %copy.92 = bf16[4,1024,512]{2,1,0:T(8,128)(2,1)} copy(bf16[4,1024,512]{1,2,0:T(8,128)(2,1)} %pad_maximum_fusion) | data formatting | bytes 8388608
  314.4 14.4 %reduce-scatter.2.cloned.1.call-done = bf16[4,64,256]{1,2,0:T(8,128)(2,1)} async-done(((bf16[32,64,256]{1,2,0:T(8,128)(2,1)}), bf16[4,64,256]{1,2,0:T(8,128)(2,1)}) %reduce-scatter.2.cloned.1.call-update) | async-done | bytes 131088 | tf_op jit(solution)/shard_map/reduce_scatter | solution.py:112
  328.8 1.1 fusion.19
  (78 shorter events, 19.7 us)
Async XLA Ops:
  7.2 295.2 %copy-start = (bf16[128,512]{1,0:T(8,128)(2,1)S(1)}, bf16[128,512]{1,0:T(8,128)(2,1)}, u32[]{:S(2)}) copy-start(bf16[128,512]{1,0:T(8,128)(2,1)} %param.24) | copy-start | bytes 393220
  7.2 60.2 %copy-start.3 = (bf16[64,256]{1,0:T(8,128)(2,1)S(1)}, bf16[64,256]{1,0:T(8,128)(2,1)}, u32[]{:S(2)}) copy-start(bf16[64,256]{1,0:T(8,128)(2,1)} %param.20) | copy-start | bytes 98308
  7.2 57.5 %all-gather.3.cloned.1.call-start = ((), (), s32[]{:S(2)}) async-start(), calls=%async_computation.2 | async-start | bytes 1081344 | tf_op jit(solution)/shard_map/all_gather | solution.py:54
  8.2 60.0 %copy-start.6 = (bf16[64,32]{0,1:T(8,128)(2,1)S(1)}, bf16[64,32]{0,1:T(8,128)(2,1)}, u32[]{:S(2)}) copy-start(bf16[64,32]{0,1:T(8,128)(2,1)} %param.17) | copy-start | bytes 12292
  11.1 136.0 %all-reduce.3.cloned.1.call-start = ((), (), s32[]{:S(2)}) async-start(), calls=%async_computation.3 | async-start | bytes 1048576 | tf_op jit(solution)/shard_map/psum | solution.py:9
  65.7 81.4 %copy-start.5 = (bf16[64,32]{0,1:T(8,128)(2,1)S(1)}, bf16[64,32]{0,1:T(8,128)(2,1)}, u32[]{:S(2)}) copy-start(bf16[64,32]{0,1:T(8,128)(2,1)} %param.16) | copy-start | bytes 12292
  66.3 82.5 %copy-start.8 = (bf16[1024,128]{1,0:T(8,128)(2,1)S(1)}, bf16[1024,128]{1,0:T(8,128)(2,1)}, u32[]{:S(2)}) copy-start(bf16[1024,128]{1,0:T(8,128)(2,1)} %param.18) | copy-start | bytes 786436
  66.3 82.5 %copy-start.11 = (f32[128]{0:T(128)S(1)}, f32[128]{0:T(128)}, u32[]{:S(2)}) copy-start(f32[128]{0:T(128)} %param.19) | copy-start | bytes 1540
  67.3 174.1 %all-gather.5.cloned.1.call-start = ((), (), s32[]{:S(2)}) async-start(), calls=%async_computation.4 | async-start | bytes 4325376 | tf_op jit(solution)/shard_map/all_gather | solution.py:58
  166.7 16.9 %copy-start.1 = (bf16[4,8,128,128]{3,2,1,0:T(8,128)(2,1)}, bf16[4,8,128,128]{3,2,1,0:T(8,128)(2,1)S(1)}, u32[]{:S(2)}) copy-start(bf16[4,8,128,128]{3,2,1,0:T(8,128)(2,1)S(1)} %get-tuple-element.41) | copy-start | bytes 3145732
  171.0 12.6 %copy-start.10 = (bf16[128,8]{0,1:T(8,128)(2,1)S(1)}, bf16[128,8]{0,1:T(8,128)(2,1)}, u32[]{:S(2)}) copy-start(bf16[128,8]{0,1:T(8,128)(2,1)} %param.22) | copy-start | bytes 6148
  174.3 125.8 %all-to-all-start = ((bf16[32,32,4,128]{3,0,2,1:T(8,128)(2,1)}), bf16[32,32,4,128]{3,0,2,1:T(8,128)(2,1)S(1)}, u32[]{:S(2)}, u32[]{:S(2)}) async-start(bf16[32,32,4,128]{3,0,2,1:T(8,128)(2,1)} %multiply_convert_fusion.1), calls=%async_computation.1 | async-start | bytes 2097152 | tf_op jit(solution)/shard_map/all_to_all | solution.py:135
  183.5 145.3 %reduce-scatter.2.cloned.1.call-start = ((), (), s32[]{:S(2)}) async-start(), calls=%async_computation.5 | async-start | bytes 2359296 | tf_op jit(solution)/shard_map/reduce_scatter | solution.py:112
  278.0 0.7 copy-start.12
  278.1 1.9 copy-start.9
  300.1 1.0 copy-start.2
  307.1 6.2 %copy-start.7 = (bf16[128,4]{0,1:T(4,128)(2,1)S(1)}, bf16[128,4]{0,1:T(4,128)(2,1)}, u32[]{:S(2)}) copy-start(bf16[128,4]{0,1:T(4,128)(2,1)} %param.25) | copy-start | bytes 3076
  313.4 16.5 %copy-start.4 = (bf16[256,64]{0,1:T(8,128)(2,1)S(1)}, bf16[256,64]{0,1:T(8,128)(2,1)}, u32[]{:S(2)}) copy-start(bf16[256,64]{0,1:T(8,128)(2,1)} %param.23) | copy-start | bytes 98308
Sparse Core Ops, SparseCore 0:
  11.3 53.4 all-gather.2
  67.9 79.1 all-reduce.2
  149.8 74.9 all-gather.4
  278.2 50.5 reduce-scatter.1
where the time goes:
time: 339 us; the launch traced here: 338 us
  blocking collectives  115 us (34%)
  waiting for transfers between devices  106 us (31%)
  local copies, waits for them, and re-layouts  56.4 us (17%)
  matrix products  22.7 us (7%)
  between operations  14.8 us (4%)
  other arithmetic  13.3 us (4%)
  starting transfers between devices  9.42 us (3%)
    pmax x1, blocking collectives, per_device(): peak_values = lax.pmax(jnp.max(logits, axis=2), 'col')  55.5 us
    all_gather x1, waiting for transfers between devices, per_device(): lax.all_gather(normalized_flat_rows, 'row', axis=1, tiled=True)  53.5 us
    all_gather x1, blocking collectives, per_device(): lax.all_gather(right_own.reshape(sequence_count, slab_length * factor_wid...  41 us
    psum x1, waiting for transfers between devices, broadcast(): return lax.psum(jnp.where(mine, shard, jnp.zeros_like(shard)), axis)  37.8 us
    unnamed x1, blocking collectives  18.6 us
    another operation x1, local copies, waits for them, and re-layouts, per_device(): value_cols.reshape(sequence_count, cols_tile, head_count, head_width)  14.8 us
    reduce_scatter x1, waiting for transfers between devices, per_device(): lax.psum_scatter(numer_part.astype(jnp.bfloat16), 'col', scatter_dimensio...  14.4 us
    unnamed x30, local copies, waits for them, and re-layouts  9.84 us
  transfers between devices with their start and end apart: 5, of which 3 were waited for; matrix products, arithmetic and copies ran while one was open for 24% of the time, Pallas kernels for 0%

commit v1 on v0

--- a/solution.py
+++ b/solution.py
@@ -6,7 +6,7 @@
 
 def broadcast(shard, axis, root):
     mine = lax.axis_index(axis) == root
-    return lax.psum(jnp.where(mine, shard, jnp.zeros_like(shard)), axis)
+    return jnp.sum(lax.all_gather(jnp.where(mine, shard, jnp.zeros_like(shard)), axis), axis=0)
 
 
 def standardize(values):

time: 339 us -> 310 us (0.914)
  waiting for transfers between devices: 106 us -> 65.7 us
  blocking collectives: 115 us -> 121 us
    psum x1 -> x0, waiting for transfers between devices: 37.8 us -> none  [broadcast(): return lax.psum(jnp.where(mine, shard, jnp.zeros_like(shard)), axis)]
    pmax x1, blocking collectives: 55.5 us -> 61.4 us  [per_device(): peak_values = lax.pmax(jnp.max(logits, axis=2), 'col')]
    unnamed x30 -> x26, local copies, waits for them, and re-layouts: 9.84 us -> 9.83 us
  transfers between devices with their start and end apart: 5 -> 5, of which waited for: 3 -> 3; matrix products, arithmetic and copies ran while one was open for 24% -> 27% of each run, Pallas kernels for 0% -> 0%
where the time goes in v1:
time: 310 us; the launch traced here: 308 us
  blocking collectives  121 us (39%)
  waiting for transfers between devices  65.7 us (21%)
  local copies, waits for them, and re-layouts  58.8 us (19%)
  matrix products  21.6 us (7%)
  other arithmetic  16 us (5%)
  between operations  14.8 us (5%)
  starting transfers between devices  9.96 us (3%)
    pmax x1, blocking collectives, per_device(): peak_values = lax.pmax(jnp.max(logits, axis=2), 'col')  61.4 us
    all_gather x1, waiting for transfers between devices, per_device(): lax.all_gather(normalized_flat_rows, 'row', axis=1, tiled=True)  53.5 us
    all_gather x1, blocking collectives, per_device(): lax.all_gather(right_own.reshape(sequence_count, slab_length * factor_wid...  43.1 us
    unnamed x1, blocking collectives  16.5 us
    another operation x1, local copies, waits for them, and re-layouts, per_device(): value_cols.reshape(sequence_count, cols_tile, head_count, head_width)  14.8 us
    reduce_scatter x1, waiting for transfers between devices, per_device(): lax.psum_scatter(numer_part.astype(jnp.bfloat16), 'col', scatter_dimensio...  11.6 us
    unnamed x26, local copies, waits for them, and re-layouts  9.83 us
    all_to_all x1, starting transfers between devices, per_device(): lax.all_to_all(shaped, 'row', split_axis=1, concat_axis=0, tiled=True)[:, 0]  9.79 us
  transfers between devices with their start and end apart: 5, of which 3 were waited for; matrix products, arithmetic and copies ran while one was open for 27% of the time, Pallas kernels for 0%

profile of v1, /device:TPU:16, one launch (start us, length us, event | category | flops | bytes accessed | tf_op | source)
XLA Modules:
  0.0 308.1 jit_solution(8056099231162806084)
XLA Ops:
  8.2 1.1 fusion.22
  9.3 1.0 fusion.23
  11.2 53.5 %all-gather.5.cloned.1.call-done = bf16[64,8192]{1,0:T(8,128)(2,1)} async-done(((bf16[64,256]{1,0:T(8,128)(2,1)}), bf16[64,8192]{1,0:T(8,128)(2,1)}) %all-gather.5.cloned.1.call-update) | async-done | bytes 1048592 | tf_op jit(solution)/shard_map/all_gather | solution.py:54
  64.7 1.7 dynamic-slice_select_fusion
  68.3 43.1 %all_gather.18 = bf16[64,4096]{0,1:T(8,128)(2,1)S(1)} all-gather(bf16[64,128]{0,1:T(8,128)(2,1)S(1)} %bitcast.145), channel_id=1, replica_groups=mesh['row'=32,'col'=8] {'row'}, dimensions={1}, use_global_device_ids=true | all-gather | bytes 540672 | tf_op jit(solution)/shard_map/all_gather | solution.py:55
  111.9 2.0 reduce_sum.62
  115.0 21.2 %while.10 = (s32[]{:T(128)}, bf16[4,8,128,128]{3,2,1,0:T(8,128)(2,1)S(1)}, bf16[4,8,128,128]{3,2,1,0:T(8,128)(2,1)}, bf16[4,64,256]{1,2,0:T(8,128)(2,1)S(1)}, bf...) while((s32[]{:T(128)}, ...), condition=%wide.region_4.5_spmd, body=%wide.region_3.4_spmd.sunk | while | flops 405274624 | bytes 12944057 | solution.py:96
  115.8 1.1 copy.116
  118.5 1.8 fusion.60
  121.1 1.1 copy.116
  123.8 1.8 fusion.60
  126.3 1.1 copy.116
  129.1 1.8 fusion.60
  131.6 1.1 copy.116
  134.4 1.8 fusion.60
  136.2 1.9 copy.89
  138.7 1.3 multiply_reduce_fusion
  140.5 3.3 %multiply_convert_fusion.1 = bf16[32,32,4,128]{3,0,2,1:T(8,128)(2,1)} fusion(f32[32,32,4,128]{3,0,2,1:T(8,128)} %bitcast.136, f32[32,32,4]{0,2,1:T(4,128)S(1)} %rsqrt.26, f32[32,32,4]{0,2,1:T(4,128)S(1)} %div.52), kind=kLoop, calls=%fused_computation.18 | loop fusion | flops 1572864 | bytes 3178496 | tf_op jit(solution)/shard_map/convert_element_type | solution.py:100
  143.8 9.8 %all-to-all-start = ((bf16[32,32,4,128]{3,0,2,1:T(8,128)(2,1)}), bf16[32,32,4,128]{3,0,2,1:T(8,128)(2,1)S(1)}, u32[]{:S(2)}, u32[]{:S(2)}) async-start(bf16[32,32,4,128]{3,0,2,1:T(8,128)(2,1)} %multiply_convert_fusion.1), calls=%async_computation.1 | async-start | bytes 2097152 | tf_op jit(solution)/shard_map/all_to_all | solution.py:135
  153.7 2.1 fusion.42
  155.8 61.4 %pmax.7 = f32[8,32]{0,1:T(8,128)S(1)} all-reduce(f32[8,32]{0,1:T(8,128)S(1)} %get-tuple-element.76), channel_id=1, replica_groups=mesh['row'=32,'col'=8] {'col'}, use_global_device_ids=true, to_apply=%region_8.9 | all-reduce | flops 256 | bytes 2048 | tf_op jit(solution)/shard_map/pmax | solution.py:102
  217.4 8.4 %copy.84 = bf16[64,32768]{0,1:T(8,128)(2,1)} copy(bf16[64,32768]{1,0:T(8,128)(2,1)} %all-gather.7.cloned.1.call-done) | data formatting | bytes 8388608 | tf_op jit(solution)/shard_map/all_gather | solution.py:58
  225.8 14.8 %copy.85 = bf16[64,128,8,32]{1,3,0,2:T(8,128)(2,1)} copy(bf16[64,128,8,32]{0,3,2,1:T(8,128)(2,1)} %bitcast.130) | data formatting | bytes 8388608 | tf_op jit(solution)/shard_map/reshape;reshape | solution.py:105
  240.6 5.4 %convert_bitcast_fusion = bf16[32,64,8,32]{0,3,1,2:T(8,128)(2,1)} fusion(bf16[64,128,8,32]{1,3,0,2:T(8,128)(2,1)} %copy.85, bf16[8,32,128,1]{2,0,1,3:T(8,128)(2,1)S(1)} %fusion.33), kind=kOutput, calls=%fused_computation.12 | convolution fusion | flops 134742016 | bytes 5308416 | tf_op jit(solution)/shard_map/hij,sjhc->ishc/dot_general | solution.py:106
  245.9 8.1 %copy.87 = bf16[32,64,8,32]{1,3,2,0:T(8,128)(2,1)} copy(bf16[32,64,8,32]{0,3,1,2:T(8,128)(2,1)} %convert_bitcast_fusion) | data formatting | bytes 2097152 | tf_op jit(solution)/shard_map/convert_element_type | solution.py:113
  256.8 16.5 %all-reduce = bf16[8,32]{0,1:T(8,128)(2,1)S(1)} all-reduce(bf16[8,32]{0,1:T(8,128)(2,1)S(1)} %fusion.32), channel_id=4, replica_groups=mesh['row'=32,'col'=8] {'col'}, use_global_device_ids=true, to_apply=%region_11.12.clone | all-reduce | flops 256 | bytes 1024
  274.3 1.3 copy.92
  275.7 1.3 convolution_bitcast_fusion
  278.0 2.4 pad_maximum_fusion
  280.4 6.2 %copy.95 = bf16[4,1024,512]{2,1,0:T(8,128)(2,1)} copy(bf16[4,1024,512]{1,2,0:T(8,128)(2,1)} %pad_maximum_fusion) | data formatting | bytes 8388608
  287.7 11.6 %reduce-scatter.2.cloned.1.call-done = bf16[4,64,256]{1,2,0:T(8,128)(2,1)} async-done(((bf16[32,64,256]{1,2,0:T(8,128)(2,1)}), bf16[4,64,256]{1,2,0:T(8,128)(2,1)}) %reduce-scatter.2.cloned.1.call-update) | async-done | bytes 131088 | tf_op jit(solution)/shard_map/reduce_scatter | solution.py:112
  299.2 1.1 fusion.19
  (99 shorter events, 22.2 us)
Async XLA Ops:
  7.2 268.5 %copy-start = (bf16[128,512]{1,0:T(8,128)(2,1)S(1)}, bf16[128,512]{1,0:T(8,128)(2,1)}, u32[]{:S(2)}) copy-start(bf16[128,512]{1,0:T(8,128)(2,1)} %param.24) | copy-start | bytes 393220
  7.2 60.9 %copy-start.7 = (bf16[64,32]{0,1:T(8,128)(2,1)S(1)}, bf16[64,32]{0,1:T(8,128)(2,1)}, u32[]{:S(2)}) copy-start(bf16[64,32]{0,1:T(8,128)(2,1)} %param.17) | copy-start | bytes 12292
  7.2 57.5 %all-gather.5.cloned.1.call-start = ((), (), s32[]{:S(2)}) async-start(), calls=%async_computation.2 | async-start | bytes 1081344 | tf_op jit(solution)/shard_map/all_gather | solution.py:54
  11.1 100.8 %all-gather.9.cloned.1.call-start = ((), (), s32[]{:S(2)}) async-start(), calls=%async_computation.5 | async-start | bytes 2359296 | tf_op jit(solution)/shard_map/all_gather | solution.py:9
  66.4 151.0 %all-gather.7.cloned.1.call-start = ((), (), s32[]{:S(2)}) async-start(), calls=%async_computation.3 | async-start | bytes 4325376 | tf_op jit(solution)/shard_map/all_gather | solution.py:58
  68.3 46.1 %copy-start.6 = (bf16[64,32]{0,1:T(8,128)(2,1)S(1)}, bf16[64,32]{0,1:T(8,128)(2,1)}, u32[]{:S(2)}) copy-start(bf16[64,32]{0,1:T(8,128)(2,1)} %param.16) | copy-start | bytes 12292
  111.4 3.7 %copy-start.12 = (f32[128]{0:T(128)S(1)}, f32[128]{0:T(128)}, u32[]{:S(2)}) copy-start(f32[128]{0:T(128)} %param.19) | copy-start | bytes 1540
  115.1 0.7 copy-start.3
  117.6 1.0 copy-start.9
  118.4 1.9 copy-start.4
  120.3 0.7 copy-start.3
  122.9 1.0 copy-start.9
  123.7 1.9 copy-start.4
  125.6 0.7 copy-start.3
  128.2 1.0 copy-start.9
  129.0 1.9 copy-start.4
  130.9 0.7 copy-start.3
  133.4 1.0 copy-start.9
  134.3 1.9 copy-start.4
  136.2 17.4 %copy-start.1 = (bf16[4,8,128,128]{3,2,1,0:T(8,128)(2,1)}, bf16[4,8,128,128]{3,2,1,0:T(8,128)(2,1)S(1)}, u32[]{:S(2)}) copy-start(bf16[4,8,128,128]{3,2,1,0:T(8,128)(2,1)S(1)} %get-tuple-element.41) | copy-start | bytes 3145732
  140.5 13.2 %copy-start.11 = (bf16[128,8]{0,1:T(8,128)(2,1)S(1)}, bf16[128,8]{0,1:T(8,128)(2,1)}, u32[]{:S(2)}) copy-start(bf16[128,8]{0,1:T(8,128)(2,1)} %param.22) | copy-start | bytes 6148
  143.8 129.5 %all-to-all-start = ((bf16[32,32,4,128]{3,0,2,1:T(8,128)(2,1)}), bf16[32,32,4,128]{3,0,2,1:T(8,128)(2,1)S(1)}, u32[]{:S(2)}, u32[]{:S(2)}) async-start(bf16[32,32,4,128]{3,0,2,1:T(8,128)(2,1)} %multiply_convert_fusion.1), calls=%async_computation.1 | async-start | bytes 2097152 | tf_op jit(solution)/shard_map/all_to_all | solution.py:135
  153.6 145.6 %reduce-scatter.2.cloned.1.call-start = ((), (), s32[]{:S(2)}) async-start(), calls=%async_computation.4 | async-start | bytes 2359296 | tf_op jit(solution)/shard_map/reduce_scatter | solution.py:112
  254.1 0.7 copy-start.13
  254.1 2.1 copy-start.10
  273.4 1.0 copy-start.2
  280.4 6.2 %copy-start.8 = (bf16[128,4]{0,1:T(4,128)(2,1)S(1)}, bf16[128,4]{0,1:T(4,128)(2,1)}, u32[]{:S(2)}) copy-start(bf16[128,4]{0,1:T(4,128)(2,1)} %param.25) | copy-start | bytes 3076
  286.6 13.7 %copy-start.5 = (bf16[256,64]{0,1:T(8,128)(2,1)S(1)}, bf16[256,64]{0,1:T(8,128)(2,1)}, u32[]{:S(2)}) copy-start(bf16[256,64]{0,1:T(8,128)(2,1)} %param.23) | copy-start | bytes 98308
Sparse Core Ops, SparseCore 0:
  11.2 53.4 all-gather.4
  67.1 44.8 all-gather.8
  114.6 78.3 all-gather.6
  254.2 44.9 reduce-scatter.1
